TPU v7x, 512 devices: a whole 4x8x8 slice. The times are simulated.
512 devices in a mesh: virt: 32 (over x, z), aux: 16 (over y, core).
Axes of the slice: x: 4, y: 8, z: 8, core: 2. Of those that a mesh axis runs over, the one named last changes fastest.
Arguments:
- three_index: bfloat16 [2400, 20480], P('aux', 'virt'), may hold values from -0.0625 to 0.0625
- eps_occ: float32 [20], replicated, may hold values from -1.5 to -0.5
- eps_virt: float32 [1024], replicated, may hold values from 0.3 to 3
Outputs:
- virt_energy: float32 [1024], P('virt')
- pair_energy: float32 [20, 20], replicated
All inputs are finite; a program needn't handle non-finite values.
Results may differ from a plain program's by a relative error of at most 0.0003.
Values may be sent and summed in bfloat16 or wider, within the bound.
No kernel may reach another device: no remote copies, remote signals or barrier semaphores. Data moves between devices by JAX's collectives and lax.ppermute only.
A program may use at most 128 MiB of HBM per device.

v0:
```python
import jax
import jax.numpy as jnp
from jax import lax
from jax.sharding import Mesh
from jax.sharding import PartitionSpec as P

VIRT = ("virt_0", "virt_1")


def joined_along(tiles, dim):
    dims = list(tiles.shape[1:])
    dims[dim] *= tiles.shape[0]
    return jnp.moveaxis(tiles, 0, dim).reshape(dims)


def gather_in_order(array, axes, sequence):
    tiles = array[None]
    for k in sequence:
        tiles = lax.all_gather(tiles, axes[k], axis=0, tiled=True)
    current = [lax.axis_size(axes[k]) for k in reversed(sequence)]
    tiles = tiles.reshape(*current, *array.shape)
    turned = sorted(range(len(sequence)), key=lambda place: sequence[len(sequence) - 1 - place])
    return tiles.transpose(*turned, *range(len(sequence), tiles.ndim)).reshape(-1, *array.shape)


def whole_of(array, axes, sequence, dim):
    return joined_along(gather_in_order(array, axes, sequence), dim)


def from_everyone(array, axis):
    copies = jnp.broadcast_to(array, (lax.axis_size(axis), *array.shape))
    return lax.all_to_all(copies, axis, split_axis=0, concat_axis=0, tiled=True)


def taken_together(array, axis):
    everything = from_everyone(array, axis)
    return jnp.sum(everything, axis=0)


def together(arrays, axis):
    ends = [0]
    for a in arrays:
        ends.append(ends[-1] + a.size)
    so_far = taken_together(jnp.concatenate([a.ravel() for a in arrays]), axis)
    return tuple((so_far[b:e].reshape(a.shape) for a, b, e in zip(arrays, ends, ends[1:])))


def on_device(three_index, eps_occ, eps_virt):
    occupied = eps_occ.shape[0]
    own_width = three_index.shape[1] // occupied
    virt_count = lax.axis_size(VIRT)
    aux_place = lax.axis_index("aux")
    virt_place = lax.axis_index(VIRT)
    narrow = lax.all_to_all(three_index, "aux", split_axis=1, concat_axis=0, tiled=True)
    partner = whole_of(narrow, VIRT, (0, 1), 1)
    stride = narrow.shape[1] // occupied
    table = eps_virt.reshape(virt_count, own_width)
    eps_other = lax.dynamic_slice_in_dim(table, aux_place * stride, stride, 1).reshape(-1)
    other_width = partner.shape[1] // occupied
    partner_cube = partner.reshape(partner.shape[0], other_width, occupied)
    eps_own = lax.dynamic_slice_in_dim(eps_virt, virt_place * own_width, own_width)
    incoming = lax.all_gather(three_index, "aux", axis=0, tiled=True)
    rows = incoming.shape[0]
    left_cube = incoming.reshape(rows, own_width, occupied)
    integrals = jnp.einsum(
        "pai,pbj->iajb", left_cube, partner_cube, preferred_element_type=jnp.float32
    )
    denominator = (
        eps_occ[:, None, None, None]
        + eps_occ[None, None, :, None]
        - eps_own[None, :, None, None]
        - eps_other[None, None, None, :]
    )
    swapped = jnp.transpose(integrals, (2, 1, 0, 3))
    energy_terms = integrals * (2.0 * integrals - swapped) / denominator
    virt_local = jnp.sum(energy_terms, axis=(0, 2, 3))
    pair_local = jnp.sum(energy_terms, axis=(1, 3))
    virt_energy, pair_column = together((virt_local, pair_local), "aux")
    pair_energy = taken_together(pair_column, VIRT)
    return (virt_energy, pair_energy)


def solution(mesh):
    split = Mesh(mesh.devices.reshape(4, 8, mesh.shape["aux"]), ("virt_0", "virt_1", "aux"))
    placed = (P("aux", VIRT), P(), P())
    return jax.shard_map(
        on_device, mesh=split, in_specs=placed, out_specs=(P(VIRT), P()), check_vma=False
    )
```

profile of v0, /device:TPU:1, one launch (start us, length us, event | category | flops | bytes accessed | tf_op | source)
XLA Modules:
  0.0 213.0 jit_solution(2634388928208436110)
XLA Ops:
  7.2 0.7 all-gather.6.cloned.1.call-update
  7.9 1.1 copy.33
  9.0 22.5 %all_to_all.27 = bf16[150,16,40]{0,2,1:T(8,128)(2,1)S(1)} all-to-all(bf16[150,16,40]{0,2,1:T(8,128)(2,1)S(1)} %bitcast.42), channel_id=1, replica_groups=mesh['virt_0'=4,'virt_1'=8,'aux'=16] {'aux'}, dimensions={1} | all-to-all | bytes 384000 | tf_op jit(solution)/shard_map/all_to_all | solution.py:54
  31.6 0.4 broadcast_in_dim.12
  32.0 13.6 %all_gather.9 = bf16[4,2400,40]{1,2,0:T(8,128)(2,1)} all-gather(bf16[1,2400,40]{1,2,0:T(8,128)(2,1)S(1)} %broadcast_in_dim.12), channel_id=1, replica_groups=mesh['virt_0'=4,'virt_1'=8,'aux'=16] {'virt_0'}, dimensions={0}, use_global_device_ids=true | all-gather | bytes 960000 | tf_op jit(solution)/shard_map/all_gather | solution.py:19
  45.7 0.8 reshape.72
  46.4 0.8 dynamic_slice.6
  47.2 0.1 constant_dynamic-slice_fusion
  47.3 0.1 sub.41
  47.4 0.8 broadcast_add_fusion
  48.2 0.1 broadcast_subtract_fusion
  48.3 10.6 %all-gather.6.cloned.1.call-done = bf16[16,150,640]{2,1,0:T(8,128)(2,1)} async-done(((bf16[1,150,640]{2,1,0:T(8,128)(2,1)}), bf16[16,150,640]{2,1,0:T(8,128)(2,1)}) %all-gather.6.cloned.1.call-update) | async-done | bytes 3072016 | tf_op jit(solution)/shard_map/all_gather | solution.py:62
  58.9 8.5 %copy.36 = bf16[16,150,640]{1,0,2:T(8,128)(2,1)} copy(bf16[16,150,640]{2,1,0:T(8,128)(2,1)} %all-gather.6.cloned.1.call-done) | data formatting | bytes 6144000 | tf_op jit(solution)/shard_map/all_gather | solution.py:62
  67.4 10.8 %reshape.71 = bf16[2400,32,20]{0,2,1:T(8,128)(2,1)} reshape(bf16[16,150,640]{1,0,2:T(8,128)(2,1)} %copy.36) | data formatting | bytes 6144000 | tf_op jit(solution)/shard_map/reshape | solution.py:64
  78.2 58.4 %all-gather.4.cloned.1.call-done = bf16[32,2400,40]{1,2,0:T(8,128)(2,1)} async-done(((bf16[4,2400,40]{1,2,0:T(8,128)(2,1)}), bf16[32,2400,40]{1,2,0:T(8,128)(2,1)}) %all-gather.4.cloned.1.call-update) | async-done | bytes 6144016 | tf_op jit(solution)/shard_map/all_gather | solution.py:19
  136.6 6.0 %copy.35 = bf16[4,8,2400,40]{2,3,1,0:T(8,128)(2,1)} copy(bf16[4,8,2400,40]{2,3,0,1:T(8,128)(2,1)} %bitcast.40) | data formatting | bytes 12288000 | tf_op jit(solution)/shard_map/transpose | solution.py:23
  142.6 10.3 %reshape_reshape.3 = bf16[2400,64,20]{0,2,1:T(8,128)(2,1)} reshape(bf16[2400,32,40]{0,2,1:T(8,128)(2,1)} %bitcast.38) | data formatting | bytes 12288000 | tf_op jit(solution)/shard_map/reshape;reshape | solution.py:60
  153.0 12.8 %fusion.2 = f32[64,20,32,20]{0,2,3,1:T(8,128)S(1)} fusion(bf16[2400,64,20,1]{0,2,1,3:T(8,128)(2,1)} %bitcast.39, bf16[2400,32,20]{0,2,1:T(8,128)(2,1)} %reshape.71), kind=kOutput, calls=%fused_computation.4 | convolution fusion | flops 3932160000 | bytes 12492800 | tf_op jit(solution)/shard_map/pai,pbj->iajb/dot_general | solution.py:65
  165.8 6.5 %fusion.7 = (f32[32]{0:T(128)S(1)}, f32[20,20]{1,0:T(8,128)S(1)}) fusion(f32[64]{0:T(128)S(1)} %sub.41, f32[20,32,20]{1,2,0:T(8,128)S(1)} %broadcast_subtract_fusion, f32[64,20,32,20]{0,2,3,1:T(8,128)S(1)} %fusion.2), kind=kLoop, calls=%fused_computation.9 | loop fusion | flops 5733968 | bytes 3329984 | tf_op jit(solution)/shard_map/reduce_sum | solution.py:76
  172.3 0.1 reshape.73
  172.4 0.1 pad_maximum_fusion
  172.5 14.8 %all_to_all.28 = f32[16,1,432]{2,1,0:T(1,128)S(1)} all-to-all(f32[16,1,432]{2,1,0:T(1,128)S(1)} %broadcast_in_dim.13), channel_id=1, replica_groups=mesh['virt_0'=4,'virt_1'=8,'aux'=16] {'aux'}, dimensions={0} | all-to-all | bytes 55296 | tf_op jit(solution)/shard_map/all_to_all | solution.py:32
  187.3 0.1 slice.7
  187.4 0.1 reshape.74
  187.5 1.0 reshape.80
  188.6 6.7 %all-to-all-start.2 = ((f32[32,1,400]{2,1,0:T(1,128)}), f32[32,1,400]{2,1,0:T(1,128)S(1)}, u32[]{:S(2)}, u32[]{:S(2)}) async-start(f32[32,1,400]{2,1,0:T(1,128)} %reshape.80), calls=%async_computation.2 | async-start | bytes 131072 | tf_op jit(solution)/shard_map/all_to_all | solution.py:32
  195.2 0.5 slice.6
  195.7 8.3 %all-to-all-done.2 = f32[32,1,400]{2,1,0:T(1,128)S(1)} async-done(((f32[32,1,400]{2,1,0:T(1,128)}), f32[32,1,400]{2,1,0:T(1,128)S(1)}, u32[]{:S(2)}, u32[]{:S(2)}) %all-to-all-start.2) | async-done | bytes 51232 | tf_op jit(solution)/shard_map/all_to_all | solution.py:32
  204.1 0.5 broadcast.38
  204.6 0.8 reduce.1
  205.4 0.2 reshape.81
  205.6 0.6 reduce_sum.39
  (7 shorter events, 0.3 us)
Async XLA Ops:
  7.2 51.8 %all-gather.6.cloned.1.call-start = ((), (), s32[]{:S(2)}) async-start(), calls=%async_computation.4 | async-start | bytes 3307520 | tf_op jit(solution)/shard_map/all_gather | solution.py:62
  7.9 128.7 %all-gather.4.cloned.1.call-start = ((), (), s32[]{:S(2)}) async-start(), calls=%async_computation.3 | async-start | bytes 7004160 | tf_op jit(solution)/shard_map/all_gather | solution.py:19
  188.6 15.5 %all-to-all-start.2 = ((f32[32,1,400]{2,1,0:T(1,128)}), f32[32,1,400]{2,1,0:T(1,128)S(1)}, u32[]{:S(2)}, u32[]{:S(2)}) async-start(f32[32,1,400]{2,1,0:T(1,128)} %reshape.80), calls=%async_computation.2 | async-start | bytes 131072 | tf_op jit(solution)/shard_map/all_to_all | solution.py:32
Sparse Core Ops, SparseCore 0:
  10.1 48.8 all-gather.5
  61.0 75.5 all-gather.3
where the time goes:
time: 214 us; the launch traced here: 213 us
  waiting for transfers between devices  78.1 us (36%)
  blocking collectives  50.9 us (24%)
  local copies, waits for them, and re-layouts  41.4 us (19%)
  between operations  14.1 us (7%)
  matrix products  12.8 us (6%)
  other arithmetic  8.98 us (4%)
  starting transfers between devices  6.74 us (3%)
    all_gather x1, waiting for transfers between devices, gather_in_order(): tiles = lax.all_gather(tiles, axes[k], axis=0, tiled=True)  58.4 us
    all_to_all x1, blocking collectives, on_device(): lax.all_to_all(three_index, 'aux', split_axis=1, concat_axis=0, tiled=True)  22.5 us
    all_to_all x1, blocking collectives, from_everyone(): return lax.all_to_all(copies, axis, split_axis=0, concat_axis=0, tiled=True)  14.8 us
    all_gather x1, blocking collectives, gather_in_order(): tiles = lax.all_gather(tiles, axes[k], axis=0, tiled=True)  13.6 us
    dot_general x1, matrix products, on_device(): jnp.einsum('pai,pbj->iajb', left_cube, partner_cube, preferred_element_ty...  12.8 us
    reshape x1, local copies, waits for them, and re-layouts, on_device(): left_cube = incoming.reshape(rows, own_width, occupied)  10.8 us
    all_gather x1, waiting for transfers between devices, on_device(): incoming = lax.all_gather(three_index, 'aux', axis=0, tiled=True)  10.6 us
    another operation x1, local copies, waits for them, and re-layouts, on_device(): partner_cube = partner.reshape(partner.shape[0], other_width, occupied)  10.3 us
  transfers between devices with their start and end apart: 3, of which 3 were waited for; matrix products, arithmetic and copies ran while one was open for 11% of the time, Pallas kernels for 0%

commit v1 on v0

v1 whole, which is shorter than its diff:
```python
import functools

import jax
import jax.numpy as jnp
from jax import lax
from jax.experimental import pallas as pl
from jax.experimental.pallas import tpu as pltpu
from jax.sharding import Mesh
from jax.sharding import PartitionSpec as P

SWAP = [(0, 1), (1, 0)]
LANES = 128


def ring_by_core(n):
    pairs = []
    for k in range(n):
        pairs.append((2 * k, 2 * ((k - 1) % n)))
        pairs.append((2 * k + 1, 2 * ((k + 1) % n) + 1))
    return pairs


def prepare(x_ref, own_ref, *, occ, own):
    width = occ * own
    rows = x_ref.shape[0]
    source = lax.broadcasted_iota(jnp.int32, (width, width), 0)
    target = lax.broadcasted_iota(jnp.int32, (width, width), 1)
    hot = ((target % own) * occ + target // own == source).astype(jnp.bfloat16)
    moved = jnp.dot(x_ref[...], hot, preferred_element_type=jnp.float32)
    own_ref[...] = jnp.zeros_like(own_ref)
    own_ref[pl.ds(0, rows), :] = moved.astype(jnp.bfloat16)


def joined(order_ref, tiles_ref, out_ref):
    count, _, part = tiles_ref.shape
    for k in range(count):
        out_ref[:, k * part : (k + 1) * part] = tiles_ref[order_ref[k]]


def transposed_groups(tiles, lane):
    a, b, c, d = tiles
    low = lane < 64
    a, c = jnp.where(low, a, pltpu.roll(c, 64, 1)), jnp.where(low, pltpu.roll(a, 64, 1), c)
    b, d = jnp.where(low, b, pltpu.roll(d, 64, 1)), jnp.where(low, pltpu.roll(b, 64, 1), d)
    even = (lane // 32) % 2 == 0
    a, b = jnp.where(even, a, pltpu.roll(b, 32, 1)), jnp.where(even, pltpu.roll(a, 96, 1), b)
    c, d = jnp.where(even, c, pltpu.roll(d, 32, 1)), jnp.where(even, pltpu.roll(c, 96, 1), d)
    return a, b, c, d


def energies(eps_ref, left_ref, b0_ref, b1_ref, la_ref, vb_ref, sum_ref, share_ref, c_ref, *, occ):
    half = b0_ref.shape[0]
    for at, b_ref in ((0, b0_ref), (half, b1_ref)):
        found = jnp.dot(b_ref[...], left_ref[...], preferred_element_type=jnp.float32)
        for t in range(c_ref.shape[0]):
            c_ref[t, pl.ds(at, half), :] = found[:, t * LANES : (t + 1) * LANES]
    lane = lax.broadcasted_iota(jnp.int32, (8, LANES), 1)
    groups = occ // 4
    vb = vb_ref[...]

    def tile(j, t):
        return c_ref[t, pl.ds(j, 8, stride=occ), :]

    share = jnp.zeros((8, LANES), jnp.float32)
    for tj in range(groups):
        for ti in range(groups):
            other = transposed_groups([tile(4 * ti + g, tj) for g in range(4)], lane)
            la = la_ref[:, ti * LANES : (ti + 1) * LANES] - vb
            for g in range(4):
                j = 4 * tj + g
                m = tile(j, ti)
                e = m * (2.0 * m - other[g]) / (la + eps_ref[j])
                share = share + e
                sum_ref[j : j + 1, ti * LANES : (ti + 1) * LANES] = jnp.sum(e, axis=0, keepdims=True)
    share_ref[...] = share


def on_device(three_index, eps_occ, eps_virt):
    occ = eps_occ.shape[0]
    rows, width = three_index.shape
    own = width // occ
    nx, nz, ny = lax.axis_size("x"), lax.axis_size("z"), lax.axis_size("y")
    parts = 2 * ny
    x, z, y, c = (lax.axis_index(k) for k in ("x", "z", "y", "c"))
    few = own // parts
    cols = few * occ
    part = -(-rows // 8) * 8
    vmem = pl.BlockSpec(memory_space=pltpu.VMEM)
    smem = pl.BlockSpec(memory_space=pltpu.SMEM)

    turned = jnp.pad(three_index, ((0, part - rows), (0, 0))).T.reshape(parts, cols, part)
    tiles = lax.all_to_all(turned, ("y", "c"), split_axis=0, concat_axis=0, tiled=True)
    sign = 1 - 2 * c
    order = [2 * y + c, 2 * y + 1 - c]
    for k in range(1, ny // 2 + 1):
        at = 2 * ((y + sign * k) % ny)
        order += [at + c, at + 1 - c]
    for k in range(1, ny // 2):
        at = 2 * ((y - sign * k) % ny)
        order += [at + 1 - c, at + c]
    order = jnp.stack(order).astype(jnp.int32)
    unit = pl.pallas_call(
        joined,
        out_shape=jax.ShapeDtypeStruct((cols, parts * part), jnp.bfloat16),
        in_specs=[smem, vmem],
        out_specs=vmem,
    )(order, tiles)

    mine = pl.pallas_call(
        functools.partial(prepare, occ=occ, own=own),
        out_shape=jax.ShapeDtypeStruct((part, width), jnp.bfloat16),
        in_specs=[vmem],
        out_specs=vmem,
    )(three_index)
    both = jnp.stack([mine, lax.ppermute(mine, "c", SWAP)])
    arrived, moving = [], both
    for _ in range(ny // 2):
        moving = lax.ppermute(moving, ("y", "c"), ring_by_core(ny))
        arrived.append(moving)
    swapped = lax.ppermute(jnp.stack(arrived[:-1]), "c", SWAP)
    left = jnp.concatenate([both, *arrived, swapped.reshape(-1, part, width)]).reshape(-1, width)

    near, far = (lax.ppermute(unit, "x", [(k, (k - d) % nx) for k in range(nx)]) for d in (1, 2))
    up, down = jnp.concatenate([unit, near]), jnp.concatenate([near, far])
    steps = nz // 2
    table = jnp.tile(eps_virt.reshape(nx, nz, parts, few), (2, 2, 1, 1))
    table = lax.dynamic_slice(table, (x, z, 2 * y + c, 0), (nx, nz, 1, few)).reshape(nx, nz, few)
    vb = [jnp.concatenate([table[0:2, k], table[1:3, -k % nz]]) for k in range(steps + 1)]
    vb = jnp.broadcast_to(jnp.stack(vb).reshape(steps + 1, 4 * few, 1), (steps + 1, 4 * few, LANES))
    eps_own = lax.dynamic_slice_in_dim(eps_virt, (x * nz + z) * own, own)
    la = jnp.broadcast_to((eps_occ[:, None] - eps_own[None, :]).reshape(1, width), (8, width))
    total, spread = None, jnp.zeros((nx, nz, few), jnp.float32)
    call = pl.pallas_call(
        functools.partial(energies, occ=occ),
        out_shape=[jax.ShapeDtypeStruct((occ, width), jnp.float32), jax.ShapeDtypeStruct((8, LANES), jnp.float32)],
        in_specs=[smem] + [vmem] * 5,
        out_specs=[vmem] * 2,
        scratch_shapes=[pltpu.VMEM((width // LANES, 4 * cols, LANES), jnp.float32)],
        cost_estimate=pl.CostEstimate(flops=8 * cols * width * parts * part, bytes_accessed=4 << 20, transcendentals=0),
    )
    for k in range(steps + 1):
        if k:
            up = lax.ppermute(up, "z", [(n, (n - 1) % nz) for n in range(nz)])
            down = lax.ppermute(down, "z", [(n, (n + 1) % nz) for n in range(nz)])
        part_sum, share = call(eps_occ, left, up, down, la, vb[k])
        weight = 0.5 if k in (0, steps) else 1.0
        part_sum = part_sum * weight
        total = part_sum if total is None else total + part_sum
        share = (jnp.sum(share, axis=1) * weight).reshape(2, 2, few)
        spread = spread.at[0:2, k].add(share[0]).at[1:3, -k % nz].add(share[1])

    cube = total.reshape(occ, occ, own)
    pairs = jnp.sum(cube, axis=2).reshape(-1)
    left_share = jnp.sum(cube, axis=(0, 1))
    wide = jnp.zeros((2 * nx, 2 * nz, own), jnp.float32)
    wide = lax.dynamic_update_slice(wide, left_share.reshape(1, 1, own), (x, z, 0)) + lax.dynamic_update_slice(
        wide, spread, (x, z, few * (2 * y + c))
    )
    spread = jnp.sum(wide.reshape(2, nx, 2, nz, own), axis=(0, 2))

    first = jnp.concatenate([spread.reshape(nx, nz * own), jnp.broadcast_to(pairs, (nx, occ * occ))], axis=1)
    first = jnp.broadcast_to(first[:, None, :], (nx, parts, first.shape[1])).reshape(nx * parts, -1)
    first = jnp.sum(lax.all_to_all(first, ("x", "y", "c"), split_axis=0, concat_axis=0, tiled=True), axis=0)
    second = jnp.concatenate(
        [first[: nz * own].reshape(nz, own), jnp.broadcast_to(first[nz * own :], (nz, occ * occ))], axis=1
    )
    second = jnp.sum(lax.all_to_all(second, "z", split_axis=0, concat_axis=0, tiled=True), axis=0)
    square = second[own:].reshape(occ, occ)
    return second[:own], square + square.T


def solution(mesh):
    split = Mesh(mesh.devices.reshape(4, 8, mesh.shape["aux"] // 2, 2), ("x", "z", "y", "c"))
    placed = (P(("y", "c"), ("x", "z")), P(), P())
    return jax.shard_map(
        on_device, mesh=split, in_specs=placed, out_specs=(P(("x", "z")), P()), check_vma=False
    )
```

time: 214 us -> 178 us (0.83)
  waiting for transfers between devices: 78.1 us -> 16.7 us
  starting transfers between devices: 6.74 us -> 59.1 us
  Pallas kernels: 0 us -> 24.7 us
  blocking collectives: 50.9 us -> 31.5 us
  matrix products: 12.8 us -> 0 us
  between operations: 14.1 us -> 1.53 us
  local copies, waits for them, and re-layouts: 41.4 us -> 29.7 us
  other arithmetic: 8.98 us -> 13.1 us
    all_gather x2 -> x0, waiting for transfers between devices: 69.1 us -> none  [the longest x1 58.4 us: gather_in_order(): tiles = lax.all_gather(tiles, axes[k], axis=0, tiled=True)]
    ppermute x0 -> x16, starting transfers between devices: none -> 55.6 us  [the longest x4 21.6 us: on_device(): up = lax.ppermute(up, 'z', [(n, (n - 1) % nz) for n in range(nz)])]
    pallas_call x0 -> x7, Pallas kernels: none -> 24.7 us  [the longest x5 20.9 us: on_device(): part_sum, share = call(eps_occ, left, up, down, la, vb[k])]
    all_gather x1 -> x0, blocking collectives: 13.6 us -> none  [gather_in_order(): tiles = lax.all_gather(tiles, axes[k], axis=0, tiled=True)]
    dot_general x1 -> x0, matrix products: 12.8 us -> none  [on_device(): jnp.einsum('pai,pbj->iajb', left_cube, partner_cube, preferred_element_ty...]
    reshape x4 -> x6, local copies, waits for them, and re-layouts: 11.7 us -> 0.53 us  [the longest x2 0.18 us: on_device(): square = second[own:].reshape(occ, occ)]
    all_gather x1 -> x0, local copies, waits for them, and re-layouts: 8.46 us -> none  [on_device(): incoming = lax.all_gather(three_index, 'aux', axis=0, tiled=True)]
    ppermute x0 -> x16, waiting for transfers between devices: none -> 8.33 us  [the longest x4 5.55 us: on_device(): moving = lax.ppermute(moving, ('y', 'c'), ring_by_core(ny))]
  transfers between devices with their start and end apart: 3 -> 17, of which waited for: 3 -> 4; matrix products, arithmetic and copies ran while one was open for 11% -> 11% of each run, Pallas kernels for 0% -> 10%
where the time goes in v1:
time: 178 us; the launch traced here: 176 us
  starting transfers between devices  59.1 us (33%)
  blocking collectives  31.5 us (18%)
  local copies, waits for them, and re-layouts  29.7 us (17%)
  Pallas kernels  24.7 us (14%)
  waiting for transfers between devices  16.7 us (9%)
  other arithmetic  13.1 us (7%)
    ppermute x4, starting transfers between devices, on_device(): up = lax.ppermute(up, 'z', [(n, (n - 1) % nz) for n in range(nz)])  21.6 us
    pallas_call x5, Pallas kernels, on_device(): part_sum, share = call(eps_occ, left, up, down, la, vb[k])  20.9 us
    all_to_all x1, blocking collectives, on_device(): lax.all_to_all(first, ('x', 'y', 'c'), split_axis=0, concat_axis=0, tiled...  20.9 us
    all_to_all x1, blocking collectives, on_device(): lax.all_to_all(second, 'z', split_axis=0, concat_axis=0, tiled=True)  10.6 us
    ppermute x1, starting transfers between devices, on_device(): both = jnp.stack([mine, lax.ppermute(mine, 'c', SWAP)])  8.87 us
    all_to_all x1, waiting for transfers between devices, on_device(): lax.all_to_all(turned, ('y', 'c'), split_axis=0, concat_axis=0, tiled=True)  8.36 us
    ppermute x4, starting transfers between devices, on_device(): moving = lax.ppermute(moving, ('y', 'c'), ring_by_core(ny))  7.89 us
    ppermute x4, starting transfers between devices, on_device(): down = lax.ppermute(down, 'z', [(n, (n + 1) % nz) for n in range(nz)])  7.69 us
  transfers between devices with their start and end apart: 17, of which 4 were waited for; matrix products, arithmetic and copies ran while one was open for 11% of the time, Pallas kernels for 10%

profile of v1, /device:TPU:1, one launch (start us, length us, event | category | flops | bytes accessed | tf_op | source)
XLA Modules:
  0.0 176.3 jit_solution(13013958068247546325)
XLA Ops:
  0.6 2.0 %shard_map.50 = bf16[152,640]{1,0:T(8,128)(2,1)} custom-call(bf16[150,640]{1,0:T(8,128)(2,1)} %x_ref.1), custom_call_target="tpu_custom_call" | custom-call | tf_op jit(solution)/shard_map/pallas_call | solution.py:109
  2.6 8.9 %collective-permute-start = (bf16[152,640]{1,0:T(8,128)(2,1)}, bf16[152,640]{1,0:T(8,128)(2,1)S(1)}, u32[]{:S(2)}, u32[]{:S(2)}) collective-permute-start(bf16[152,640]{1,0:T(8,128)(2,1)} %shard_map.50), channel_id=1, source_target_pairs={{0,1},{1,0},{2,3},{3,2},{4,5},{5,4},{6,7},{7,6},{8,9},{9,8},{10,11... | collective-permute-start | bytes 583688 | tf_op jit(solution)/shard_map/ppermute | solution.py:115
  13.4 3.4 %all-to-all-start = ((bf16[16,40,152]{2,1,0:T(8,128)(2,1)}), bf16[16,40,152]{2,1,0:T(8,128)(2,1)S(1)}, u32[]{:S(2)}, u32[]{:S(2)}) async-start(bf16[16,40,152]{2,1,0:T(8,128)(2,1)} %bitcast.24), calls=%async_computation | async-start | bytes 655360 | tf_op jit(solution)/shard_map/all_to_all | solution.py:92
  21.6 8.4 %all-to-all-done.tiles_ref = bf16[16,40,152]{2,1,0:T(8,128)(2,1)S(1)} async-done(((bf16[16,40,152]{2,1,0:T(8,128)(2,1)}), bf16[16,40,152]{2,1,0:T(8,128)(2,1)S(1)}, u32[]{:S(2)}, u32[]{:S(2)}) %all-to-all-start) | async-done | bytes 194592 | tf_op jit(solution)/shard_map/all_to_all | solution.py:92
  30.7 1.8 %shard_map.51 = bf16[40,2432]{1,0:T(8,128)(2,1)} custom-call(s32[16]{0:T(128)} %stack.101.order_ref, bf16[16,40,152]{2,1,0:T(8,128)(2,1)} %copy-done.6), custom_call_target="tpu_custom_call" | custom-call | tf_op jit(solution)/shard_map/pallas_call | solution.py:102
  32.5 2.6 %collective-permute-start.6 = (bf16[40,2432]{1,0:T(8,128)(2,1)}, bf16[40,2432]{1,0:T(8,128)(2,1)S(1)}, u32[]{:S(2)}, u32[]{:S(2)}) collective-permute-start(bf16[40,2432]{1,0:T(8,128)(2,1)} %shard_map.51), channel_id=1, source_target_pairs={{0,384},{128,0},{256,128},{384,256},{1,385},{129,1},{257,129},{385... | collective-permute-start | bytes 583688 | tf_op jit(solution)/shard_map/ppermute | solution.py:123
  35.2 1.9 %collective-permute-start.1 = (bf16[2,152,640]{2,1,0:T(8,128)(2,1)S(1)}, bf16[2,152,640]{2,1,0:T(8,128)(2,1)S(1)}, u32[]{:S(2)}, u32[]{:S(2)}) collective-permute-start(bf16[2,152,640]{2,1,0:T(8,128)(2,1)S(1)} %pad_maximum_fusion.1), channel_id=1, source_target_pairs={{0,14},{1,3},{2,0},{3,5},{4,2},{5,7},{6,4},{7,9},{8,6},{9,11},{10,... | collective-permute-start | bytes 1167368 | tf_op jit(solution)/shard_map/ppermute | solution.py:118
  37.4 2.4 %collective-permute-start.7 = (bf16[40,2432]{1,0:T(8,128)(2,1)}, bf16[40,2432]{1,0:T(8,128)(2,1)S(1)}, u32[]{:S(2)}, u32[]{:S(2)}) collective-permute-start(bf16[40,2432]{1,0:T(8,128)(2,1)} %shard_map.51), channel_id=1, source_target_pairs={{0,256},{128,384},{256,0},{384,128},{1,257},{129,385},{257,1},{385... | collective-permute-start | bytes 583688 | tf_op jit(solution)/shard_map/ppermute | solution.py:123
  42.1 9.6 %collective-permute-start.8 = (bf16[80,2432]{1,0:T(8,128)(2,1)S(1)}, bf16[80,2432]{1,0:T(8,128)(2,1)}, u32[]{:S(2)}, u32[]{:S(2)}) collective-permute-start(bf16[80,2432]{1,0:T(8,128)(2,1)S(1)} %pad_maximum_fusion.2.b0_ref), channel_id=1, source_target_pairs={{0,112},{16,0},{32,16},{48,32},{64,48},{80,64},{96,80},{112,96},{1... | collective-permute-start | bytes 1167368 | tf_op jit(solution)/shard_map/ppermute | solution.py:143
  51.8 2.1 %collective-permute-start.2 = (bf16[2,152,640]{2,1,0:T(8,128)(2,1)S(1)}, bf16[2,152,640]{2,1,0:T(8,128)(2,1)S(1)}, u32[]{:S(2)}, u32[]{:S(2)}) collective-permute-start(bf16[2,152,640]{2,1,0:T(8,128)(2,1)S(1)} %collective-permute-done.1), channel_id=1, source_target_pairs={{0,14},{1,3},{2,0},{3,5},{4,2},{5,7},{6,4},{7,9},{8,6},{9,11},{10,... | collective-permute-start | bytes 1167368 | tf_op jit(solution)/shard_map/ppermute | solution.py:118
  54.0 1.9 %collective-permute-start.9 = (bf16[80,2432]{1,0:T(8,128)(2,1)S(1)}, bf16[80,2432]{1,0:T(8,128)(2,1)}, u32[]{:S(2)}, u32[]{:S(2)}) collective-permute-start(bf16[80,2432]{1,0:T(8,128)(2,1)S(1)} %constant_dynamic-update-slice_fusion.7.b1_ref), channel_id=1, source_target_pairs={{0,16},{16,32},{32,48},{48,64},{64,80},{80,96},{96,112},{112,0},{1... | collective-permute-start | bytes 1167368 | tf_op jit(solution)/shard_map/ppermute | solution.py:144
  55.9 5.5 %collective-permute-done.2 = bf16[2,152,640]{2,1,0:T(8,128)(2,1)S(1)} collective-permute-done((bf16[2,152,640]{2,1,0:T(8,128)(2,1)S(1)}, bf16[2,152,640]{2,1,0:T(8,128)(2,1)S(1)}, u32[]{:S(2)}, u32[]{:S(2)}) %collective-permute-start.2) | collective-permute-done | bytes 389152 | tf_op jit(solution)/shard_map/ppermute | solution.py:118
  61.5 1.9 %collective-permute-start.3 = (bf16[2,152,640]{2,1,0:T(8,128)(2,1)S(1)}, bf16[2,152,640]{2,1,0:T(8,128)(2,1)S(1)}, u32[]{:S(2)}, u32[]{:S(2)}) collective-permute-start(bf16[2,152,640]{2,1,0:T(8,128)(2,1)S(1)} %collective-permute-done.2), channel_id=1, source_target_pairs={{0,14},{1,3},{2,0},{3,5},{4,2},{5,7},{6,4},{7,9},{8,6},{9,11},{10,... | collective-permute-start | bytes 1167368 | tf_op jit(solution)/shard_map/ppermute | solution.py:118
  65.1 4.5 %collective-permute-start.10 = (bf16[80,2432]{1,0:T(8,128)(2,1)}, bf16[80,2432]{1,0:T(8,128)(2,1)}, u32[]{:S(2)}, u32[]{:S(2)}) collective-permute-start(bf16[80,2432]{1,0:T(8,128)(2,1)} %collective-permute-done.8.b0_ref), channel_id=1, source_target_pairs={{0,112},{16,0},{32,16},{48,32},{64,48},{80,64},{96,80},{112,96},{1... | collective-permute-start | bytes 1167368 | tf_op jit(solution)/shard_map/ppermute | solution.py:143
  69.6 1.9 %collective-permute-start.11 = (bf16[80,2432]{1,0:T(8,128)(2,1)}, bf16[80,2432]{1,0:T(8,128)(2,1)}, u32[]{:S(2)}, u32[]{:S(2)}) collective-permute-start(bf16[80,2432]{1,0:T(8,128)(2,1)} %collective-permute-done.9.b1_ref), channel_id=1, source_target_pairs={{0,16},{16,32},{32,48},{48,64},{64,80},{80,96},{96,112},{112,0},{1... | collective-permute-start | bytes 1167368 | tf_op jit(solution)/shard_map/ppermute | solution.py:144
  72.7 4.6 %collective-permute-start.5 = (bf16[3,2,152,640]{3,2,1,0:T(8,128)(2,1)}, bf16[3,2,152,640]{3,2,1,0:T(8,128)(2,1)}, u32[]{:S(2)}, u32[]{:S(2)}) collective-permute-start(bf16[3,2,152,640]{3,2,1,0:T(8,128)(2,1)} %pad_maximum_fusion), channel_id=1, source_target_pairs={{0,1},{1,0},{2,3},{3,2},{4,5},{5,4},{6,7},{7,6},{8,9},{9,8},{10,11... | collective-permute-start | bytes 3502088 | tf_op jit(solution)/shard_map/ppermute | solution.py:120
  78.6 3.9 %collective-permute-start.12 = (bf16[80,2432]{1,0:T(8,128)(2,1)}, bf16[80,2432]{1,0:T(8,128)(2,1)}, u32[]{:S(2)}, u32[]{:S(2)}) collective-permute-start(bf16[80,2432]{1,0:T(8,128)(2,1)} %collective-permute-done.10.b0_ref), channel_id=1, source_target_pairs={{0,112},{16,0},{32,16},{48,32},{64,48},{80,64},{96,80},{112,96},{1... | collective-permute-start | bytes 1167368 | tf_op jit(solution)/shard_map/ppermute | solution.py:143
  82.5 1.9 %collective-permute-start.13 = (bf16[80,2432]{1,0:T(8,128)(2,1)}, bf16[80,2432]{1,0:T(8,128)(2,1)}, u32[]{:S(2)}, u32[]{:S(2)}) collective-permute-start(bf16[80,2432]{1,0:T(8,128)(2,1)} %collective-permute-done.11.b1_ref), channel_id=1, source_target_pairs={{0,16},{16,32},{32,48},{48,64},{64,80},{80,96},{96,112},{112,0},{1... | collective-permute-start | bytes 1167368 | tf_op jit(solution)/shard_map/ppermute | solution.py:144
  84.4 1.9 %collective-permute-start.4 = (bf16[2,152,640]{2,1,0:T(8,128)(2,1)}, bf16[2,152,640]{2,1,0:T(8,128)(2,1)S(1)}, u32[]{:S(2)}, u32[]{:S(2)}) collective-permute-start(bf16[2,152,640]{2,1,0:T(8,128)(2,1)} %copy-done.5), channel_id=1, source_target_pairs={{0,14},{1,3},{2,0},{3,5},{4,2},{5,7},{6,4},{7,9},{8,6},{9,11},{10,... | collective-permute-start | bytes 1167368 | tf_op jit(solution)/shard_map/ppermute | solution.py:118
  90.9 3.6 %collective-permute-start.14 = (bf16[80,2432]{1,0:T(8,128)(2,1)}, bf16[80,2432]{1,0:T(8,128)(2,1)}, u32[]{:S(2)}, u32[]{:S(2)}) collective-permute-start(bf16[80,2432]{1,0:T(8,128)(2,1)} %collective-permute-done.12.b0_ref), channel_id=1, source_target_pairs={{0,112},{16,0},{32,16},{48,32},{64,48},{80,64},{96,80},{112,96},{1... | collective-permute-start | bytes 1167368 | tf_op jit(solution)/shard_map/ppermute | solution.py:143
  94.5 1.9 %collective-permute-start.15 = (bf16[80,2432]{1,0:T(8,128)(2,1)}, bf16[80,2432]{1,0:T(8,128)(2,1)}, u32[]{:S(2)}, u32[]{:S(2)}) collective-permute-start(bf16[80,2432]{1,0:T(8,128)(2,1)} %collective-permute-done.13.b1_ref), channel_id=1, source_target_pairs={{0,16},{16,32},{32,48},{48,64},{64,80},{80,96},{96,112},{112,0},{1... | collective-permute-start | bytes 1167368 | tf_op jit(solution)/shard_map/ppermute | solution.py:144
  99.7 4.2 %shard_map.52 = (f32[20,640]{1,0:T(8,128)}, f32[8,128]{1,0:T(8,128)}) custom-call(f32[20]{0:T(128)} %eps_ref.9, bf16[2432,640]{1,0:T(8,128)(2,1)} %bitcast.54, bf16[80,2432]{1,0:T(8,128)(2,1)} %copy-done.2, bf16[80,2432]{1,0:T(8,128)(2,1)} %copy-done.7, f32[8,640]{1,0:T(8,128)} %broadcast_in_dim.47.la_ref, f32[8,128]{1,0:T(8,128)} %broadcast_in_dim.49.vb_ref), custom_call_target="tpu_custom_call" | custom-call | flops 498073600 | bytes 4194304 | tf_op jit(solution)/shard_map/pallas_call | solution.py:145
  104.5 4.2 %shard_map.55 = (f32[20,640]{1,0:T(8,128)}, f32[8,128]{1,0:T(8,128)}) custom-call(f32[20]{0:T(128)} %eps_ref.9, bf16[2432,640]{1,0:T(8,128)(2,1)} %bitcast.55, bf16[80,2432]{1,0:T(8,128)(2,1)} %collective-permute-done.12.b0_ref, bf16[80,2432]{1,0:T(8,128)(2,1)} %collective-permute-done.13.b1_ref, f32[8,640]{1,0:T(8,128)} %broadcast_in_dim.47.la_ref, ...), custom_call_target="tpu_custom_call" | custom-call | flops 498073600 | bytes 4194304 | tf_op jit(solution)/shard_map/pallas_call | solution.py:145
  109.4 4.2 %shard_map.54 = (f32[20,640]{1,0:T(8,128)}, f32[8,128]{1,0:T(8,128)}) custom-call(f32[20]{0:T(128)} %eps_ref.9, bf16[2432,640]{1,0:T(8,128)(2,1)} %bitcast.56, bf16[80,2432]{1,0:T(8,128)(2,1)} %collective-permute-done.10.b0_ref, bf16[80,2432]{1,0:T(8,128)(2,1)} %collective-permute-done.11.b1_ref, f32[8,640]{1,0:T(8,128)} %broadcast_in_dim.47.la_ref, ...), custom_call_target="tpu_custom_call" | custom-call | flops 498073600 | bytes 4194304 | tf_op jit(solution)/shard_map/pallas_call | solution.py:145
  114.2 4.2 %shard_map.53 = (f32[20,640]{1,0:T(8,128)}, f32[8,128]{1,0:T(8,128)}) custom-call(f32[20]{0:T(128)} %eps_ref.9, bf16[2432,640]{1,0:T(8,128)(2,1)} %bitcast.57, bf16[80,2432]{1,0:T(8,128)(2,1)} %collective-permute-done.8.b0_ref, bf16[80,2432]{1,0:T(8,128)(2,1)} %collective-permute-done.9.b1_ref, f32[8,640]{1,0:T(8,128)} %broadcast_in_dim.47.la_ref, ...), custom_call_target="tpu_custom_call" | custom-call | flops 498073600 | bytes 4194304 | tf_op jit(solution)/shard_map/pallas_call | solution.py:145
  119.1 4.2 %shard_map.56 = (f32[20,640]{1,0:T(8,128)}, f32[8,128]{1,0:T(8,128)}) custom-call(f32[20]{0:T(128)} %eps_ref.9, bf16[2432,640]{1,0:T(8,128)(2,1)} %bitcast.58, bf16[80,2432]{1,0:T(8,128)(2,1)} %collective-permute-done.14.b0_ref, bf16[80,2432]{1,0:T(8,128)(2,1)} %collective-permute-done.15.b1_ref, f32[8,640]{1,0:T(8,128)} %broadcast_in_dim.47.la_ref, ...), custom_call_target="tpu_custom_call" | custom-call | flops 498073600 | bytes 4194304 | tf_op jit(solution)/shard_map/pallas_call | solution.py:145
  128.0 1.8 %add_select_fusion.2 = f32[2,1,2]{2,0,1:T(2,128)S(1)} fusion(f32[2,1,2]{2,0,1:T(2,128)S(1)} %reshape.588, f32[4,8,2]{2,0,1:T(4,128)S(1)} %scatter-add.39, s32[]{:T(128)} %bitcast.41, s32[]{:T(128)} %bitcast.42, pred[]{:T(512)} %get-tuple-element.144), kind=kLoop, calls=%fused_computation.30 | loop fusion | flops 8 | bytes 57 | tf_op jit(solution)/shard_map/select.14
  131.5 1.8 %add_select_fusion.1 = f32[2,1,2]{2,0,1:T(2,128)S(1)} fusion(f32[2,1,2]{2,0,1:T(2,128)S(1)} %reshape.592, f32[4,8,2]{2,0,1:T(4,128)S(1)} %scatter-add.41, s32[]{:T(128)} %bitcast.43, s32[]{:T(128)} %bitcast.44, pred[]{:T(512)} %get-tuple-element.143), kind=kLoop, calls=%fused_computation.29 | loop fusion | flops 8 | bytes 57 | tf_op jit(solution)/shard_map/select.16
  135.8 2.0 %add_select_fusion = f32[2,1,2]{2,0,1:T(2,128)S(1)} fusion(f32[2,1,2]{2,0,1:T(2,128)S(1)} %slice.471, f32[4,8,2]{2,0,1:T(4,128)S(1)} %scatter-add.45, s32[]{:T(128)} %bitcast.45, s32[]{:T(128)} %bitcast.46, pred[]{:T(512)} %get-tuple-element.142), kind=kLoop, calls=%fused_computation.28 | loop fusion | flops 8 | bytes 57 | tf_op jit(solution)/shard_map/select.18
  139.7 2.6 %add.243 = f32[8,16,32]{2,0,1:T(8,128)S(1)} dynamic-update-slice(f32[8,16,32]{2,0,1:T(8,128)S(1)} %dynamic_update_slice.8, f32[4,8,2]{2,0,1:T(4,128)S(1)} %dynamic-slice_add_fusion, s32[]{:T(128)S(6)} %select_n.58, s32[]{:T(128)S(6)} %select_n.59, s32[]{:T(128)S(6)} %select_n.61) | dynamic-update-slice | bytes 516 | tf_op jit(solution)/shard_map/add | solution.py:156
  143.0 20.9 %all_to_all.23 = f32[64,1,656]{2,1,0:T(1,128)S(1)} all-to-all(f32[64,1,656]{2,1,0:T(1,128)S(1)} %all_to_all.16), channel_id=1, replica_groups=mesh['x'=4,'z'=8,'y'=8,'c'=2] {'x','y','c'}, dimensions={0} | all-to-all | bytes 335872 | tf_op jit(solution)/shard_map/all_to_all | solution.py:163
  164.2 10.6 %all_to_all.24 = f32[8,1,432]{2,1,0:T(1,128)S(1)} all-to-all(f32[8,1,432]{2,1,0:T(1,128)S(1)} %all_to_all.18), channel_id=1, replica_groups=mesh['x'=4,'z'=8,'y'=8,'c'=2] {'z'}, dimensions={0} | all-to-all | bytes 27648 | tf_op jit(solution)/shard_map/all_to_all | solution.py:167
  (176 shorter events, 37.4 us)
Async XLA Ops:
  0.6 64.4 %copy-start.12 = (f32[20]{0:T(128)S(1)}, f32[20]{0:T(128)}, u32[]{:S(2)}) copy-start(f32[20]{0:T(128)} %eps_ref.9) | copy-start | bytes 244
  2.6 32.5 %copy-start.1 = (bf16[152,640]{1,0:T(8,128)(2,1)S(1)}, bf16[152,640]{1,0:T(8,128)(2,1)}, u32[]{:S(2)}) copy-start(bf16[152,640]{1,0:T(8,128)(2,1)} %shard_map.50) | copy-start | bytes 583684
  2.6 32.5 %collective-permute-start = (bf16[152,640]{1,0:T(8,128)(2,1)}, bf16[152,640]{1,0:T(8,128)(2,1)S(1)}, u32[]{:S(2)}, u32[]{:S(2)}) collective-permute-start(bf16[152,640]{1,0:T(8,128)(2,1)} %shard_map.50), channel_id=1, source_target_pairs={{0,1},{1,0},{2,3},{3,2},{4,5},{5,4},{6,7},{7,6},{8,9},{9,8},{10,11... | collective-permute-start | bytes 583688 | tf_op jit(solution)/shard_map/ppermute | solution.py:115
  13.4 16.6 %all-to-all-start = ((bf16[16,40,152]{2,1,0:T(8,128)(2,1)}), bf16[16,40,152]{2,1,0:T(8,128)(2,1)S(1)}, u32[]{:S(2)}, u32[]{:S(2)}) async-start(bf16[16,40,152]{2,1,0:T(8,128)(2,1)} %bitcast.24), calls=%async_computation | async-start | bytes 655360 | tf_op jit(solution)/shard_map/all_to_all | solution.py:92
  17.7 60.1 %copy-start.17 = (s32[3]{0:T(128)S(1)}, s32[3]{0:T(128)}, u32[]{:S(2)}) copy-start(s32[3]{0:T(128)} %constant.358.clone.1) | copy-start | bytes 40
  32.5 8.6 %collective-permute-start.6 = (bf16[40,2432]{1,0:T(8,128)(2,1)}, bf16[40,2432]{1,0:T(8,128)(2,1)S(1)}, u32[]{:S(2)}, u32[]{:S(2)}) collective-permute-start(bf16[40,2432]{1,0:T(8,128)(2,1)} %shard_map.51), channel_id=1, source_target_pairs={{0,384},{128,0},{256,128},{384,256},{1,385},{129,1},{257,129},{385... | collective-permute-start | bytes 583688 | tf_op jit(solution)/shard_map/ppermute | solution.py:123
  35.2 16.5 %collective-permute-start.1 = (bf16[2,152,640]{2,1,0:T(8,128)(2,1)S(1)}, bf16[2,152,640]{2,1,0:T(8,128)(2,1)S(1)}, u32[]{:S(2)}, u32[]{:S(2)}) collective-permute-start(bf16[2,152,640]{2,1,0:T(8,128)(2,1)S(1)} %pad_maximum_fusion.1), channel_id=1, source_target_pairs={{0,14},{1,3},{2,0},{3,5},{4,2},{5,7},{6,4},{7,9},{8,6},{9,11},{10,... | collective-permute-start | bytes 1167368 | tf_op jit(solution)/shard_map/ppermute | solution.py:118
  37.4 16.6 %collective-permute-start.7 = (bf16[40,2432]{1,0:T(8,128)(2,1)}, bf16[40,2432]{1,0:T(8,128)(2,1)S(1)}, u32[]{:S(2)}, u32[]{:S(2)}) collective-permute-start(bf16[40,2432]{1,0:T(8,128)(2,1)} %shard_map.51), channel_id=1, source_target_pairs={{0,256},{128,384},{256,0},{384,128},{1,257},{129,385},{257,1},{385... | collective-permute-start | bytes 583688 | tf_op jit(solution)/shard_map/ppermute | solution.py:123
  42.1 35.7 %copy-start.2 = (bf16[80,2432]{1,0:T(8,128)(2,1)}, bf16[80,2432]{1,0:T(8,128)(2,1)S(1)}, u32[]{:S(2)}) copy-start(bf16[80,2432]{1,0:T(8,128)(2,1)S(1)} %pad_maximum_fusion.2.b0_ref) | copy-start | bytes 1167364
  42.1 23.0 %collective-permute-start.8 = (bf16[80,2432]{1,0:T(8,128)(2,1)S(1)}, bf16[80,2432]{1,0:T(8,128)(2,1)}, u32[]{:S(2)}, u32[]{:S(2)}) collective-permute-start(bf16[80,2432]{1,0:T(8,128)(2,1)S(1)} %pad_maximum_fusion.2.b0_ref), channel_id=1, source_target_pairs={{0,112},{16,0},{32,16},{48,32},{64,48},{80,64},{96,80},{112,96},{1... | collective-permute-start | bytes 1167368 | tf_op jit(solution)/shard_map/ppermute | solution.py:143
  51.8 26.0 %copy-start.3 = (bf16[2,152,640]{2,1,0:T(8,128)(2,1)}, bf16[2,152,640]{2,1,0:T(8,128)(2,1)S(1)}, u32[]{:S(2)}) copy-start(bf16[2,152,640]{2,1,0:T(8,128)(2,1)S(1)} %collective-permute-done.1) | copy-start | bytes 1167364
  51.8 9.7 %collective-permute-start.2 = (bf16[2,152,640]{2,1,0:T(8,128)(2,1)S(1)}, bf16[2,152,640]{2,1,0:T(8,128)(2,1)S(1)}, u32[]{:S(2)}, u32[]{:S(2)}) collective-permute-start(bf16[2,152,640]{2,1,0:T(8,128)(2,1)S(1)} %collective-permute-done.1), channel_id=1, source_target_pairs={{0,14},{1,3},{2,0},{3,5},{4,2},{5,7},{6,4},{7,9},{8,6},{9,11},{10,... | collective-permute-start | bytes 1167368 | tf_op jit(solution)/shard_map/ppermute | solution.py:118
  54.0 23.8 %copy-start.7 = (bf16[80,2432]{1,0:T(8,128)(2,1)}, bf16[80,2432]{1,0:T(8,128)(2,1)S(1)}, u32[]{:S(2)}) copy-start(bf16[80,2432]{1,0:T(8,128)(2,1)S(1)} %constant_dynamic-update-slice_fusion.7.b1_ref) | copy-start | bytes 1167364
  54.0 15.6 %collective-permute-start.9 = (bf16[80,2432]{1,0:T(8,128)(2,1)S(1)}, bf16[80,2432]{1,0:T(8,128)(2,1)}, u32[]{:S(2)}, u32[]{:S(2)}) collective-permute-start(bf16[80,2432]{1,0:T(8,128)(2,1)S(1)} %constant_dynamic-update-slice_fusion.7.b1_ref), channel_id=1, source_target_pairs={{0,16},{16,32},{32,48},{48,64},{64,80},{80,96},{96,112},{112,0},{1... | collective-permute-start | bytes 1167368 | tf_op jit(solution)/shard_map/ppermute | solution.py:144
  61.5 16.3 %copy-start.4 = (bf16[2,152,640]{2,1,0:T(8,128)(2,1)}, bf16[2,152,640]{2,1,0:T(8,128)(2,1)S(1)}, u32[]{:S(2)}) copy-start(bf16[2,152,640]{2,1,0:T(8,128)(2,1)S(1)} %collective-permute-done.2) | copy-start | bytes 1167364
  61.5 10.1 %collective-permute-start.3 = (bf16[2,152,640]{2,1,0:T(8,128)(2,1)S(1)}, bf16[2,152,640]{2,1,0:T(8,128)(2,1)S(1)}, u32[]{:S(2)}, u32[]{:S(2)}) collective-permute-start(bf16[2,152,640]{2,1,0:T(8,128)(2,1)S(1)} %collective-permute-done.2), channel_id=1, source_target_pairs={{0,14},{1,3},{2,0},{3,5},{4,2},{5,7},{6,4},{7,9},{8,6},{9,11},{10,... | collective-permute-start | bytes 1167368 | tf_op jit(solution)/shard_map/ppermute | solution.py:118
  65.1 13.5 %collective-permute-start.10 = (bf16[80,2432]{1,0:T(8,128)(2,1)}, bf16[80,2432]{1,0:T(8,128)(2,1)}, u32[]{:S(2)}, u32[]{:S(2)}) collective-permute-start(bf16[80,2432]{1,0:T(8,128)(2,1)} %collective-permute-done.8.b0_ref), channel_id=1, source_target_pairs={{0,112},{16,0},{32,16},{48,32},{64,48},{80,64},{96,80},{112,96},{1... | collective-permute-start | bytes 1167368 | tf_op jit(solution)/shard_map/ppermute | solution.py:143
  69.6 12.9 %collective-permute-start.11 = (bf16[80,2432]{1,0:T(8,128)(2,1)}, bf16[80,2432]{1,0:T(8,128)(2,1)}, u32[]{:S(2)}, u32[]{:S(2)}) collective-permute-start(bf16[80,2432]{1,0:T(8,128)(2,1)} %collective-permute-done.9.b1_ref), channel_id=1, source_target_pairs={{0,16},{16,32},{32,48},{48,64},{64,80},{80,96},{96,112},{112,0},{1... | collective-permute-start | bytes 1167368 | tf_op jit(solution)/shard_map/ppermute | solution.py:144
  71.5 6.3 %copy-start.5 = (bf16[2,152,640]{2,1,0:T(8,128)(2,1)}, bf16[2,152,640]{2,1,0:T(8,128)(2,1)S(1)}, u32[]{:S(2)}) copy-start(bf16[2,152,640]{2,1,0:T(8,128)(2,1)S(1)} %collective-permute-done.3) | copy-start | bytes 1167364
  72.7 23.8 %collective-permute-start.5 = (bf16[3,2,152,640]{3,2,1,0:T(8,128)(2,1)}, bf16[3,2,152,640]{3,2,1,0:T(8,128)(2,1)}, u32[]{:S(2)}, u32[]{:S(2)}) collective-permute-start(bf16[3,2,152,640]{3,2,1,0:T(8,128)(2,1)} %pad_maximum_fusion), channel_id=1, source_target_pairs={{0,1},{1,0},{2,3},{3,2},{4,5},{5,4},{6,7},{7,6},{8,9},{9,8},{10,11... | collective-permute-start | bytes 3502088 | tf_op jit(solution)/shard_map/ppermute | solution.py:120
  78.6 12.3 %collective-permute-start.12 = (bf16[80,2432]{1,0:T(8,128)(2,1)}, bf16[80,2432]{1,0:T(8,128)(2,1)}, u32[]{:S(2)}, u32[]{:S(2)}) collective-permute-start(bf16[80,2432]{1,0:T(8,128)(2,1)} %collective-permute-done.10.b0_ref), channel_id=1, source_target_pairs={{0,112},{16,0},{32,16},{48,32},{64,48},{80,64},{96,80},{112,96},{1... | collective-permute-start | bytes 1167368 | tf_op jit(solution)/shard_map/ppermute | solution.py:143
  82.5 12.0 %collective-permute-start.13 = (bf16[80,2432]{1,0:T(8,128)(2,1)}, bf16[80,2432]{1,0:T(8,128)(2,1)}, u32[]{:S(2)}, u32[]{:S(2)}) collective-permute-start(bf16[80,2432]{1,0:T(8,128)(2,1)} %collective-permute-done.11.b1_ref), channel_id=1, source_target_pairs={{0,16},{16,32},{32,48},{48,64},{64,80},{80,96},{96,112},{112,0},{1... | collective-permute-start | bytes 1167368 | tf_op jit(solution)/shard_map/ppermute | solution.py:144
  84.4 12.1 %collective-permute-start.4 = (bf16[2,152,640]{2,1,0:T(8,128)(2,1)}, bf16[2,152,640]{2,1,0:T(8,128)(2,1)S(1)}, u32[]{:S(2)}, u32[]{:S(2)}) collective-permute-start(bf16[2,152,640]{2,1,0:T(8,128)(2,1)} %copy-done.5), channel_id=1, source_target_pairs={{0,14},{1,3},{2,0},{3,5},{4,2},{5,7},{6,4},{7,9},{8,6},{9,11},{10,... | collective-permute-start | bytes 1167368 | tf_op jit(solution)/shard_map/ppermute | solution.py:118
  90.9 27.5 %collective-permute-start.14 = (bf16[80,2432]{1,0:T(8,128)(2,1)}, bf16[80,2432]{1,0:T(8,128)(2,1)}, u32[]{:S(2)}, u32[]{:S(2)}) collective-permute-start(bf16[80,2432]{1,0:T(8,128)(2,1)} %collective-permute-done.12.b0_ref), channel_id=1, source_target_pairs={{0,112},{16,0},{32,16},{48,32},{64,48},{80,64},{96,80},{112,96},{1... | collective-permute-start | bytes 1167368 | tf_op jit(solution)/shard_map/ppermute | solution.py:143
  94.5 23.9 %collective-permute-start.15 = (bf16[80,2432]{1,0:T(8,128)(2,1)}, bf16[80,2432]{1,0:T(8,128)(2,1)}, u32[]{:S(2)}, u32[]{:S(2)}) collective-permute-start(bf16[80,2432]{1,0:T(8,128)(2,1)} %collective-permute-done.13.b1_ref), channel_id=1, source_target_pairs={{0,16},{16,32},{32,48},{48,64},{64,80},{80,96},{96,112},{112,0},{1... | collective-permute-start | bytes 1167368 | tf_op jit(solution)/shard_map/ppermute | solution.py:144
  114.2 9.1 %copy-start.8 = (f32[20,640]{1,0:T(8,128)S(1)}, f32[20,640]{1,0:T(8,128)}, u32[]{:S(2)}) copy-start(f32[20,640]{1,0:T(8,128)} %get-tuple-element.132) | copy-start | bytes 153604
  114.2 9.1 %copy-start.9 = (f32[20,640]{1,0:T(8,128)S(1)}, f32[20,640]{1,0:T(8,128)}, u32[]{:S(2)}) copy-start(f32[20,640]{1,0:T(8,128)} %get-tuple-element.135) | copy-start | bytes 153604
  114.2 9.1 %copy-start.10 = (f32[20,640]{1,0:T(8,128)S(1)}, f32[20,640]{1,0:T(8,128)}, u32[]{:S(2)}) copy-start(f32[20,640]{1,0:T(8,128)} %get-tuple-element.134) | copy-start | bytes 153604
  118.4 5.9 %copy-start.15 = (f32[8,128]{1,0:T(8,128)S(1)}, f32[8,128]{1,0:T(8,128)}, u32[]{:S(2)}) copy-start(f32[8,128]{1,0:T(8,128)} %get-tuple-element.137) | copy-start | bytes 12292
  118.4 6.3 %copy-start.16 = (f32[8,128]{1,0:T(8,128)S(1)}, f32[8,128]{1,0:T(8,128)}, u32[]{:S(2)}) copy-start(f32[8,128]{1,0:T(8,128)} %get-tuple-element.138) | copy-start | bytes 12292
  118.4 9.3 %copy-start.14 = (f32[8,128]{1,0:T(8,128)S(1)}, f32[8,128]{1,0:T(8,128)}, u32[]{:S(2)}) copy-start(f32[8,128]{1,0:T(8,128)} %get-tuple-element.139) | copy-start | bytes 12292
  118.4 12.8 %copy-start.13 = (f32[8,128]{1,0:T(8,128)S(1)}, f32[8,128]{1,0:T(8,128)}, u32[]{:S(2)}) copy-start(f32[8,128]{1,0:T(8,128)} %get-tuple-element.140) | copy-start | bytes 12292
  (3 other events, 7.3 us)
